TPU v7x, 512 devices: a whole 4x8x8 slice. The times are simulated.
512 devices in a mesh: group: 8 (over y), shard: 64 (over z, x, core).
Axes of the slice: x: 4, y: 8, z: 8, core: 2. Of those that a mesh axis runs over, the one named last changes fastest.
Arguments:
- item_features: bfloat16 [65536, 1024], P(('group', 'shard')), may hold values from -24 to 24
- tower_weight: bfloat16 [1024, 1024], replicated, may hold values from -0.1875 to 0.1875
- item_table: bfloat16 [65536, 1024], P(('group', 'shard')), may hold values from -4 to 4
- owner: int32 [65536, 1], P(('group', 'shard')), may hold values from 0 to 63; in each aligned block of 128 rows (0 to 127, 128 to 255, ...) at most 4 rows name the same one
- table_slot: int32 [65536], P(('group', 'shard')), may hold values from 0 to 127
- pair_users: int32 [65536, 2], P(('group', 'shard')), may hold values from 0 to 255
- user_comps: bfloat16 [2048, 1024], P(('group', 'shard')), may hold values from -0.5 to 0.5
- user_gates: bfloat16 [2048, 64], P(('group', 'shard')), may hold values from -6 to 6
Outputs:
- tower_grad: float32 [1024, 1024], P('shard')
- table_grad: float32 [65536, 1024], P(('group', 'shard'))
- user_comp_grad: float32 [2048, 1024], P(('group', 'shard'))
- user_gate_grad: float32 [2048, 64], P(('group', 'shard'))
Inputs may be any that keep to these rules, and one draw needn't show every extreme that they name: Among the rows of one device, no owner is named more than 4 times, a bound that some block reaches. `pair_users`: user numbers within the item's own group.
All inputs are finite; a program needn't handle non-finite values.
Results may differ from a plain program's by a relative error of at most 0.0042.
Values may be sent and summed in bfloat16 or wider, within the bound.
A program may use at most 64 MiB of HBM per device.

v0:
```python
import functools

import jax
import jax.numpy as jnp
from jax import lax
from jax.experimental import pallas as pl
from jax.experimental.pallas import tpu as pltpu
from jax.sharding import PartitionSpec as P

MESH = pl.DeviceIdType.MESH
COMPS = 8
CAP = 4
CORES = 2
QUARTERS = 4
BLOCK = CAP * QUARTERS
GROUP = 16
LANES = 128
F32, BF16 = jnp.float32, jnp.bfloat16


def nn(a, b):
    return lax.dot_general(a, b, (((1,), (0,)), ((), ())), preferred_element_type=F32)


def nt(a, b):
    return lax.dot_general(a, b, (((1,), (1,)), ((), ())), preferred_element_type=F32)


def tn(a, b):
    return lax.dot_general(a, b, (((0,), (0,)), ((), ())), preferred_element_type=F32)


def ones_where(condition):
    return jnp.where(condition, 1.0, 0.0).astype(BF16)


def iota(shape, dim):
    return lax.broadcasted_iota(jnp.int32, shape, dim)


def halves(values):
    high = values.astype(BF16)
    return high, (values - high.astype(F32)).astype(BF16)


def sigmoid(values):
    return 1.0 / (1.0 + jnp.exp(-values))


def kernel(
    groups, shards, nx,
    ids_ref, x_ref, w_ref, table_ref, own_users_ref,
    tower_out, table_out, users_out, gates_out,
    head_send, head_recv, users_all, xt, xt_recv, embedded, slope, rows_send, rows_recv,
    picked, gates_wide, combined, d_comb, d_pre, d_pre_recv, d_users, d_gates,
    users_part, users_part_recv, tower_part, tower_x, tower_mid, tower_z, tower_low, tower_y,
    users_half, users_x, users_mid, users_z, back_send, back_recv,
    send_sems, recv_sems,
):
    n, d = x_ref.shape
    slots = table_ref.shape[0]
    width = d // QUARTERS
    rows = shards * BLOCK
    half = rows // CORES
    nz = shards // (nx * CORES)
    depth = d // shards
    chips = shards // CORES
    g, s = lax.axis_index("group"), lax.axis_index("shard")
    core = lax.rem(s, CORES)
    chip = lax.div(s, CORES)
    x, z = lax.rem(chip, nx), lax.div(chip, nx)

    def at(z_to, x_to, core_to):
        return (g, (z_to * nx + x_to) * CORES + core_to)

    partner = at(z, x, 1 - core)

    def copy(number, source, target, device):
        return pltpu.make_async_remote_copy(
            src_ref=source, dst_ref=target,
            send_sem=send_sems.at[number], recv_sem=recv_sems.at[number],
            device_id=device, device_id_type=MESH,
        )

    def wait_recv(number, whole):
        copy(number, whole, whole, partner).wait_recv()

    def wait_send(number, whole):
        copy(number, whole, whole, partner).wait_send()

    def loop(low, high, step):
        def run(i, carry):
            step(i)
            return carry
        lax.fori_loop(low, high, run, 0)

    def block(i, size):
        return pl.ds(pl.multiple_of(i * size, size), size)

    barrier = pltpu.get_barrier_semaphore()
    loop(1, shards, lambda k: pl.semaphore_signal(
        barrier, inc=1, device_id=(g, lax.rem(s + k, shards)), device_id_type=MESH))
    loop(1, groups, lambda k: pl.semaphore_signal(
        barrier, inc=1, device_id=(lax.rem(g + k, groups), s), device_id_type=MESH))

    target = ids_ref[0:1, :]
    slot = ids_ref[1:2, :]
    to_owner = jnp.where(iota((shards, n), 0) == target, 1.0, 0.0)
    earlier = ones_where(iota((n, n), 0) < iota((n, n), 1))
    before = nn(to_owner.astype(BF16), earlier)
    within = jnp.sum(before * to_owner, axis=0, keepdims=True).astype(jnp.int32)
    place_row = (target * CAP + within) * QUARTERS
    eye = iota((n, n), 0) == iota((n, n), 1)

    def as_column(row):
        wide = jnp.where(eye, row.astype(F32), 0.0)
        return jnp.sum(wide, axis=1, keepdims=True).astype(jnp.int32)

    place_col = as_column(place_row)
    wanted = (to_owner * (slot + 1).astype(F32)).astype(BF16)
    turn = ones_where(iota((LANES, n), 0) == within)
    head_send[...] = nt(wanted, turn).reshape(shards, 1, LANES)

    for tile in range(d // LANES):
        turned = x_ref[:, tile * LANES:(tile + 1) * LANES].astype(F32).T.astype(BF16)
        for piece in range(max(1, LANES // depth)):
            size = min(depth, LANES)
            first = tile * LANES + piece * size
            holder, rest = divmod(first, depth)
            c_h, chip_h = holder % CORES, holder // CORES
            row = ((chip_h % nx) * nz + chip_h // nx) * depth + rest
            xt[c_h, row:row + size, :] = turned[piece * size:(piece + 1) * size]

    own = core * chips + x * nz + z
    users_all[block(own, BLOCK), :] = own_users_ref[...]

    pl.semaphore_wait(barrier, shards - 1 + groups - 1)

    def send_head(k):
        p = lax.rem(s + k, shards)
        copy(0, head_send.at[p], head_recv.at[s], (g, p)).start()
    loop(1, shards, send_head)
    head_recv[s] = head_send[s]

    def send_users(k):
        p = lax.rem(chip + k, chips)
        copy(1, own_users_ref, users_all.at[block(own, BLOCK)], (g, p * CORES + core)).start()
    loop(1, chips, send_users)
    copy(2, xt.at[1 - core], xt_recv, partner).start()

    def tower(q):
        columns = block(q, width)
        pre = nn(x_ref[...], w_ref[:, columns])
        share = 0.5 + 0.5 * lax.erf(pre * (0.5 ** 0.5))
        embedded[block(q, n), :] = (pre * share).astype(BF16)
        slope[:, columns] = share + pre * (0.3989422804014327 * jnp.exp(-0.5 * pre * pre))
    loop(0, QUARTERS, tower)

    wait_recv(0, head_recv.at[pl.ds(0, shards - 1)])
    heads = head_recv[...].reshape(shards, LANES).astype(BF16)

    tile_rows = min(256, rows)

    def answer(t):
        index = iota((tile_rows, shards), 0) + t * tile_rows
        spread = nn(ones_where((index >> 4) == iota((tile_rows, shards), 1)), heads)
        index = iota((tile_rows, LANES), 0) + t * tile_rows
        mine = jnp.where(((index >> 2) & 3) == iota((tile_rows, LANES), 1), spread, 0.0)
        asked = jnp.sum(mine, axis=1, keepdims=True).astype(jnp.int32) - 1
        quarter = index[:, 0:1] & 3
        out = jnp.zeros((tile_rows, width), F32)
        for q in range(QUARTERS):
            key = jnp.where(quarter == q, asked, -1)
            pick = ones_where(key == iota((tile_rows, slots), 1))
            out = out + nn(pick, table_ref[:, q * width:(q + 1) * width])
        rows_send[block(t, tile_rows), :] = out.astype(BF16)
    loop(0, rows // tile_rows, answer)

    def send_rows(k):
        p = lax.rem(s + k, shards)
        copy(3, rows_send.at[block(p, BLOCK)], rows_recv.at[block(s, BLOCK)], (g, p)).start()
    loop(1, shards, send_rows)
    rows_recv[block(s, BLOCK), :] = rows_send[block(s, BLOCK), :]

    others = pl.ds(0, half - BLOCK)
    wait_recv(1, users_all.at[others])
    mine = pl.ds(pl.multiple_of(core * half, half), half)
    copy(4, users_all.at[mine], users_all.at[mine], partner).start()

    held = tn(heads, ones_where((iota((shards, rows), 1) >> 4) == iota((shards, rows), 0)))
    lane = iota((LANES, rows), 1)
    held = jnp.where(((lane >> 2) & 3) == iota((LANES, rows), 0), held, 0.0)
    asked_row = jnp.sum(held, axis=0, keepdims=True).astype(jnp.int32) - 1

    def user_key(row):
        user, holder = row & 3, row >> 2
        c_u, chip_u = holder & 1, holder >> 1
        where = c_u * chips + (chip_u & (nx - 1)) * nz + (chip_u >> (nx.bit_length() - 1))
        return (where * CAP + user) * QUARTERS

    key_rows = [user_key(ids_ref[2 + side:3 + side, :]) for side in range(2)]
    key_cols = [as_column(row) for row in key_rows]
    expand = ones_where(iota((LANES, width), 0) == (iota((LANES, width), 1) >> 4))
    wait_recv(4, users_all.at[mine])
    for side in range(2):
        def pick_users(q):
            pick = ones_where(key_cols[side] + q == iota((n, rows), 1))
            got = nn(pick, users_all[...]).astype(BF16)
            here = block(side * QUARTERS + q, n)
            picked[here, :] = got[:, :width]
            gates_wide[here, :] = nn(got[:, width:], expand).astype(BF16)
        loop(0, QUARTERS, pick_users)

    wait_recv(3, rows_recv.at[pl.ds(0, rows - BLOCK)])

    def combine(q):
        pick = ones_where(place_col + q == iota((n, rows), 1))
        here = block(q, n)
        combined[here, :] = embedded[here, :].astype(F32) + nn(pick, rows_recv[...])
    loop(0, QUARTERS, combine)

    def spot(index, b):
        return pl.ds(pl.multiple_of(index * n + b * GROUP, GROUP), GROUP)

    def lanes_of(p):
        return slice((p & 1) * LANES, (p & 1) * LANES + LANES)

    def stack(ref, b, sides):
        return jnp.concatenate(
            [ref[spot(side * QUARTERS + (p >> 1), b), lanes_of(p)] for side in range(sides) for p in range(COMPS)],
            axis=0)

    pairs = COMPS * GROUP

    def pair_loss(b):
        comb = stack(combined, b, 1)
        scale = lax.rsqrt(jnp.mean(comb * comb, axis=1, keepdims=True) + 1e-06)
        normed = comb * scale
        n_high, n_low = halves(normed)
        users = stack(picked, b, 2)
        gates = stack(gates_wide, b, 2).astype(F32)
        logits = nt(users, n_high) + nt(users, n_low)
        same = (iota((2 * pairs, pairs), 0) & (GROUP - 1)) == (iota((2 * pairs, pairs), 1) & (GROUP - 1))
        weights = sigmoid(gates + logits)
        terms = jnp.where(same, weights * logits, 0.0)
        factors = []
        for side in range(2):
            total = terms[side * pairs:side * pairs + GROUP]
            for p in range(1, COMPS):
                total = total + terms[side * pairs + p * GROUP:side * pairs + (p + 1) * GROUP]
            score = 0.125 * jnp.sum(total, axis=1, keepdims=True)
            factor = sigmoid(score) if side else -sigmoid(-score)
            factors += [0.125 * factor] * COMPS
        factor = jnp.where(same, jnp.concatenate(factors, axis=0), 0.0)
        bend = logits * (weights * (1.0 - weights))
        dg_high, dg_low = halves(factor * bend)
        dl = factor * (weights + bend)
        dl_high, dl_low = halves(dl)
        d_normed = tn(dl_high, users) + tn(dl_low, users)
        du_high, du_low = halves(nn(dl_high, n_high) + nn(dl_low, n_high) + nn(dl_high, n_low))
        d_row = scale * (d_normed - normed * jnp.mean(d_normed * normed, axis=1, keepdims=True))
        d_row = d_row.astype(BF16)
        for p in range(COMPS):
            part = d_row[p * GROUP:(p + 1) * GROUP]
            d_comb[spot(p >> 1, b), lanes_of(p)] = part
            item, column = block(b, GROUP), slice(p * LANES, (p + 1) * LANES)
            d_pre[item, column] = (part.astype(F32) * slope[item, column]).astype(BF16)
        for side in range(2):
            for p in range(COMPS):
                here = spot(side * QUARTERS + (p >> 1), b)
                part = slice(side * pairs + p * GROUP, side * pairs + (p + 1) * GROUP)
                lane0 = (p & 1) * LANES
                d_users[here, lane0:lane0 + LANES] = du_high[part]
                d_users[here, width + lane0:width + lane0 + LANES] = du_low[part]
                d_gates[here, lane0:lane0 + LANES] = dg_high[part]
                d_gates[here, width + lane0:width + lane0 + LANES] = dg_low[part]
    loop(0, n // GROUP, pair_loss)

    copy(5, d_pre, d_pre_recv, partner).start()

    def give_back(t):
        index = iota((tile_rows, n), 0) + t * tile_rows
        put = jnp.concatenate([ones_where(index == place_row + q) for q in range(QUARTERS)], axis=1)
        back_send[block(t, tile_rows), :] = nn(put, d_comb[...]).astype(BF16)
    loop(0, rows // tile_rows, give_back)

    def send_back(k):
        p = lax.rem(s + k, shards)
        copy(6, back_send.at[block(p, BLOCK)], back_recv.at[block(s, BLOCK)], (g, p)).start()
    loop(1, shards, send_back)
    back_recv[block(s, BLOCK), :] = back_send[block(s, BLOCK), :]

    wait_recv(2, xt_recv)
    wait_recv(5, d_pre_recv)
    wide = nz * depth

    def tower_rows(i):
        here = block(i, wide)
        total = nn(xt[core, here, :], d_pre[...]) + nn(xt_recv[here, :], d_pre_recv[...])
        tower_part[here, :] = total.astype(BF16)
    loop(0, nx, tower_rows)

    def send_x(k):
        to = lax.rem(x + k, nx)
        copy(8, tower_part.at[block(to, wide)], tower_x.at[x], at(z, to, core)).start()
    loop(1, nx, send_x)

    def squeeze(i):
        here = block(i, n)
        high, low = halves(nt(d_gates[here, :width], expand) + nt(d_gates[here, width:], expand))
        d_users[here, 2 * width:2 * width + LANES] = high
        d_users[here, 2 * width + LANES:] = low
    loop(0, 2 * QUARTERS, squeeze)

    tile_users = min(128, rows)

    def sum_users(t):
        index = iota((tile_users, n), 0) + t * tile_users
        put = jnp.concatenate(
            [ones_where(index == key_rows[side] + q) for side in range(2) for q in range(QUARTERS)], axis=1)
        total = nn(put, d_users[...])
        here = block(t, tile_users)
        users_part[here, :width] = total[:, :width] + total[:, width:2 * width]
        users_part[here, width:] = total[:, 2 * width:2 * width + LANES] + total[:, 2 * width + LANES:]
    loop(0, rows // tile_users, sum_users)
    theirs = pl.ds(pl.multiple_of((1 - core) * half, half), half)
    copy(7, users_part.at[theirs], users_part_recv, partner).start()
    wait_recv(7, users_part_recv)
    users_half[...] = (users_part[mine, :] + users_part_recv[...]).astype(BF16)
    tall = nz * BLOCK

    def send_ux(k):
        to = lax.rem(x + k, nx)
        copy(9, users_half.at[block(to, tall)], users_x.at[x], at(z, to, core)).start()
    loop(1, nx, send_ux)

    wait_recv(8, tower_x.at[pl.ds(0, nx - 1)])
    total = tower_part[block(x, wide), :].astype(F32)
    for k in range(1, nx):
        total = total + tower_x[lax.rem(x + k, nx)].astype(F32)
    tower_mid[...] = total.astype(BF16)

    def send_z(k):
        to = lax.rem(z + k, nz)
        copy(10, tower_mid.at[block(to, depth)], tower_z.at[z], at(to, x, core)).start()
    loop(1, nz, send_z)

    wait_recv(9, users_x.at[pl.ds(0, nx - 1)])
    total = users_half[block(x, tall), :].astype(F32)
    for k in range(1, nx):
        total = total + users_x[lax.rem(x + k, nx)].astype(F32)
    users_mid[...] = total.astype(BF16)

    def send_uz(k):
        to = lax.rem(z + k, nz)
        copy(11, users_mid.at[block(to, BLOCK)], users_z.at[z], at(to, x, core)).start()
    loop(1, nz, send_uz)

    wait_recv(6, back_recv.at[pl.ds(0, rows - BLOCK)])
    quarter_row = iota((1, rows), 1) & 3
    for q in range(QUARTERS):
        key = jnp.where(quarter_row == q, asked_row, -1)
        pick = ones_where(key == iota((slots, rows), 0))
        table_out[:, q * width:(q + 1) * width] = nn(pick, back_recv[...])

    wait_recv(10, tower_z.at[pl.ds(0, nz - 1)])
    total = tower_mid[block(z, depth), :].astype(F32)
    for k in range(1, nz):
        total = total + tower_z[lax.rem(z + k, nz)].astype(F32)
    tower_low[...] = total.astype(BF16)

    def send_y(k):
        copy(12, tower_low, tower_y.at[g], (lax.rem(g + k, groups), s)).start()
    loop(1, groups, send_y)

    wait_recv(11, users_z.at[pl.ds(0, nz - 1)])
    total = users_mid[block(z, BLOCK), :].astype(F32)
    for k in range(1, nz):
        total = total + users_z[lax.rem(z + k, nz)].astype(F32)
    users_out[...] = total[:, :width]
    gates_out[...] = total[:, width:]

    tower_y[g] = tower_low[...]
    wait_recv(12, tower_y.at[pl.ds(0, groups - 1)])
    total = tower_y[0].astype(F32)
    for k in range(1, groups):
        total = total + tower_y[k].astype(F32)
    tower_out[...] = total

    wait_send(0, head_send.at[pl.ds(0, shards - 1)])
    wait_send(1, users_all.at[others])
    wait_send(2, xt_recv)
    wait_send(3, rows_send.at[pl.ds(0, rows - BLOCK)])
    wait_send(4, users_all.at[mine])
    wait_send(5, d_pre)
    wait_send(6, back_send.at[pl.ds(0, rows - BLOCK)])
    wait_send(7, users_part_recv)
    wait_send(8, tower_x.at[pl.ds(0, nx - 1)])
    wait_send(9, users_x.at[pl.ds(0, nx - 1)])
    wait_send(10, tower_z.at[pl.ds(0, nz - 1)])
    wait_send(11, users_z.at[pl.ds(0, nz - 1)])
    wait_send(12, tower_y.at[pl.ds(0, groups - 1)])


def local(item_features, tower_weight, item_table, owner, table_slot, pair_users, user_comps, user_gates):
    groups, shards = lax.axis_size("group"), lax.axis_size("shard")
    nx = 4 if shards >= 64 else 2
    nz = shards // (nx * CORES)
    n, d = item_features.shape
    slots = item_table.shape[0]
    held = user_comps.shape[0]
    width = d // QUARTERS
    rows = shards * BLOCK
    half = rows // CORES
    depth = d // shards
    across = width + LANES
    ids = jnp.concatenate(
        [owner.reshape(1, n), table_slot.reshape(1, n), pair_users.T], axis=0)
    gates = user_gates.reshape(held * QUARTERS, -1)
    own_users = jnp.concatenate(
        [user_comps.reshape(BLOCK, width), jnp.pad(gates, ((0, 0), (0, LANES - gates.shape[1])))], axis=1)
    scratch = [
        ((shards, 1, LANES), F32), ((shards, 1, LANES), F32),
        ((rows, across), BF16),
        ((CORES, d // 2, n), BF16), ((d // 2, n), BF16),
        ((QUARTERS * n, width), BF16), ((n, d), F32),
        ((rows, width), BF16), ((rows, width), BF16),
        ((2 * QUARTERS * n, width), BF16), ((2 * QUARTERS * n, width), BF16),
        ((QUARTERS * n, width), F32), ((QUARTERS * n, width), BF16),
        ((n, d), BF16), ((n, d), BF16),
        ((2 * QUARTERS * n, 2 * across), BF16), ((2 * QUARTERS * n, 2 * width), BF16),
        ((rows, across), F32), ((half, across), F32),
        ((d // 2, d), BF16), ((nx, nz * depth, d), BF16), ((nz * depth, d), BF16),
        ((nz, depth, d), BF16), ((depth, d), BF16), ((groups, depth, d), BF16),
        ((half, across), BF16), ((nx, nz * BLOCK, across), BF16), ((nz * BLOCK, across), BF16),
        ((nz, BLOCK, across), BF16),
        ((rows, width), BF16), ((rows, width), BF16),
    ]
    whole = pl.BlockSpec(memory_space=pltpu.VMEM)
    tower_grad, table_grad, user_rows, gate_rows = pl.pallas_call(
        functools.partial(kernel, groups, shards, nx),
        out_shape=(
            jax.ShapeDtypeStruct((depth, d), F32),
            jax.ShapeDtypeStruct((slots, d), F32),
            jax.ShapeDtypeStruct((BLOCK, width), F32),
            jax.ShapeDtypeStruct((BLOCK, LANES), F32),
        ),
        in_specs=[whole] * 5,
        out_specs=(whole,) * 4,
        scratch_shapes=[pltpu.VMEM(shape, kind) for shape, kind in scratch]
        + [pltpu.SemaphoreType.DMA((13,)), pltpu.SemaphoreType.DMA((13,))],
        compiler_params=pltpu.CompilerParams(
            collective_id=0, has_side_effects=True, vmem_limit_bytes=56 * 1024 * 1024),
    )(ids, item_features, tower_weight, item_table, own_users)
    user_comp_grad = user_rows.reshape(held, d)
    user_gate_grad = gate_rows[:, : gates.shape[1]].reshape(held, -1)
    return tower_grad, table_grad, user_comp_grad, user_gate_grad


def solution(mesh):
    spread = P(("group", "shard"), None)
    return jax.shard_map(
        local,
        mesh=mesh,
        in_specs=(spread, P(), spread, spread, P(("group", "shard")), spread, spread, spread),
        out_specs=(P("shard", None), spread, spread, spread),
        check_vma=False,
    )
```

profile of v0, /device:TPU:2, one launch (start us, length us, event | category | flops | bytes accessed | tf_op | source)
XLA Modules:
  0.0 98.8 jit_solution(17292483615869895399)
XLA Ops:
  0.6 1.3 %pad_add_fusion.ids_ref = s32[4,128]{1,0:T(4,128)} fusion(s32[2,128]{1,0:T(2,128)} %bitcast.5, s32[1,128]{1,0:T(1,128)} %bitcast.6, s32[1,128]{1,0:T(1,128)} %bitcast.7), kind=kLoop, calls=%fused_computation.3 | loop fusion | flops 1024 | bytes 4096 | tf_op jit(solution)/shard_map/concatenate | solution.py:417
  1.9 0.8 reshape.29
  2.7 0.7 reshape.28
  3.4 0.6 fusion.1.own_users_ref
  4.0 88.8 %shard_map.111 = (f32[16,1024]{1,0:T(8,128)}, f32[128,1024]{1,0:T(8,128)}, f32[16,256]{1,0:T(8,128)}, f32[16,128]{1,0:T(8,128)}) custom-call(s32[4,128]{1,0:T(4,128)} %pad_add_fusion.ids_ref, bf16[128,1024]{1,0:T(8,128)(2,1)} %x_ref.1, bf16[1024,1024]{1,0:T(8,128)(2,1)} %w_ref.1, bf16[128,1024]{1,0:T(8,128)(2,1)} %table_ref.1, ...), custom_call_target="tpu_custom_call" | custom-call | tf_op jit(solution)/shard_map/pallas_call | solution.py:440
  92.8 1.4 %reshape.31 = f32[4,64]{1,0:T(4,128)} reshape(f32[16,16]{1,0:T(8,128)} %bitcast.4) | data formatting | bytes 2048 | tf_op jit(solution)/shard_map/reshape | solution.py:456
  94.1 1.3 %reshape.30 = f32[4,1024]{1,0:T(4,128)} reshape(f32[16,256]{1,0:T(8,128)} %get-tuple-element.10) | data formatting | bytes 32768 | tf_op jit(solution)/shard_map/reshape | solution.py:455
  95.5 1.5 %copy.14 = f32[16,1024]{1,0:T(8,128)} copy(f32[16,1024]{1,0:T(8,128)} %get-tuple-element.16) | data formatting | bytes 131072
  96.9 1.9 %copy.15 = f32[128,1024]{1,0:T(8,128)} copy(f32[128,1024]{1,0:T(8,128)} %get-tuple-element.17) | data formatting | bytes 1048576
where the time goes:
time: 99.2 us; the launch traced here: 98.8 us
  Pallas kernels  88.8 us (90%)
  local copies, waits for them, and re-layouts  7.51 us (8%)
  other arithmetic  1.89 us (2%)
    pallas_call x1, Pallas kernels, local(): pl.pallas_call(functools.partial(kernel, groups, shards, nx), out_shape=(...  88.8 us
    unnamed x2, local copies, waits for them, and re-layouts  3.36 us

commit v1 on v0

--- a/solution.py
+++ b/solution.py
@@ -49,13 +49,13 @@
 
 def kernel(
     groups, shards, nx,
-    ids_ref, x_ref, w_ref, table_ref, own_users_ref,
+    owner_ref, slot_ref, pair_ref, x_ref, w_hbm, table_ref, comps_ref, gates_ref,
     tower_out, table_out, users_out, gates_out,
-    head_send, head_recv, users_all, xt, xt_recv, embedded, slope, rows_send, rows_recv,
+    w_ref, own_rows, own_users, head_send, head_recv, users_all, xt, xt_recv, embedded, slope, rows_send, rows_recv,
     picked, gates_wide, combined, d_comb, d_pre, d_pre_recv, d_users, d_gates,
     users_part, users_part_recv, tower_part, tower_x, tower_mid, tower_z, tower_low, tower_y,
     users_half, users_x, users_mid, users_z, back_send, back_recv,
-    send_sems, recv_sems,
+    send_sems, recv_sems, head_sems, w_sem,
 ):
     n, d = x_ref.shape
     slots = table_ref.shape[0]
@@ -97,14 +97,16 @@
     def block(i, size):
         return pl.ds(pl.multiple_of(i * size, size), size)
 
+    load_w = pltpu.make_async_copy(w_hbm, w_ref, w_sem)
+    load_w.start()
     barrier = pltpu.get_barrier_semaphore()
     loop(1, shards, lambda k: pl.semaphore_signal(
         barrier, inc=1, device_id=(g, lax.rem(s + k, shards)), device_id_type=MESH))
     loop(1, groups, lambda k: pl.semaphore_signal(
         barrier, inc=1, device_id=(lax.rem(g + k, groups), s), device_id_type=MESH))
 
-    target = ids_ref[0:1, :]
-    slot = ids_ref[1:2, :]
+    target = owner_ref[...]
+    slot = slot_ref[...]
     to_owner = jnp.where(iota((shards, n), 0) == target, 1.0, 0.0)
     earlier = ones_where(iota((n, n), 0) < iota((n, n), 1))
     before = nn(to_owner.astype(BF16), earlier)
@@ -121,6 +123,40 @@
     turn = ones_where(iota((LANES, n), 0) == within)
     head_send[...] = nt(wanted, turn).reshape(shards, 1, LANES)
 
+    own_rows[:, width:] = jnp.zeros((BLOCK, LANES), F32)
+    gate_lane = iota((1, COMPS * COMPS), 1)
+    own_comps, own_gates = comps_ref[...].astype(F32), gates_ref[...].astype(F32)
+    for u in range(CAP):
+        for q in range(QUARTERS):
+            row = u * QUARTERS + q
+            own_rows[row:row + 1, :width] = own_comps[u:u + 1, q * width:(q + 1) * width]
+            own_rows[row:row + 1, width:width + COMPS * COMPS] = jnp.where(
+                (gate_lane >> 4) == q, own_gates[u:u + 1, :], 0.0)
+    own_users[...] = own_rows[...].astype(BF16)
+    own = core * chips + x * nz + z
+    users_all[block(own, BLOCK), :] = own_users[...]
+
+    pl.semaphore_wait(barrier, shards - 1 + groups - 1)
+
+    column = nx * CORES
+
+    def head(away, p):
+        return pltpu.make_async_remote_copy(
+            src_ref=head_send.at[p], dst_ref=head_recv.at[s],
+            send_sem=send_sems.at[0], recv_sem=head_sems.at[away],
+            device_id=(g, p), device_id_type=MESH,
+        )
+
+    def send_head(k):
+        p = lax.rem(s + k, shards)
+        head(lax.rem(z - lax.div(p, column) + nz, nz), p).start()
+    loop(1, shards, send_head)
+    head_recv[s] = head_send[s]
+
+    def send_users(k):
+        p = lax.rem(chip + k, chips)
+        copy(1, own_users, users_all.at[block(own, BLOCK)], (g, p * CORES + core)).start()
+    loop(1, chips, send_users)
     for tile in range(d // LANES):
         turned = x_ref[:, tile * LANES:(tile + 1) * LANES].astype(F32).T.astype(BF16)
         for piece in range(max(1, LANES // depth)):
@@ -131,22 +167,9 @@
             row = ((chip_h % nx) * nz + chip_h // nx) * depth + rest
             xt[c_h, row:row + size, :] = turned[piece * size:(piece + 1) * size]
 
-    own = core * chips + x * nz + z
-    users_all[block(own, BLOCK), :] = own_users_ref[...]
-
-    pl.semaphore_wait(barrier, shards - 1 + groups - 1)
-
-    def send_head(k):
-        p = lax.rem(s + k, shards)
-        copy(0, head_send.at[p], head_recv.at[s], (g, p)).start()
-    loop(1, shards, send_head)
-    head_recv[s] = head_send[s]
-
-    def send_users(k):
-        p = lax.rem(chip + k, chips)
-        copy(1, own_users_ref, users_all.at[block(own, BLOCK)], (g, p * CORES + core)).start()
-    loop(1, chips, send_users)
     copy(2, xt.at[1 - core], xt_recv, partner).start()
+
+    load_w.wait()
 
     def tower(q):
         columns = block(q, width)
@@ -156,30 +179,46 @@
         slope[:, columns] = share + pre * (0.3989422804014327 * jnp.exp(-0.5 * pre * pre))
     loop(0, QUARTERS, tower)
 
-    wait_recv(0, head_recv.at[pl.ds(0, shards - 1)])
-    heads = head_recv[...].reshape(shards, LANES).astype(BF16)
-
     tile_rows = min(256, rows)
-
-    def answer(t):
-        index = iota((tile_rows, shards), 0) + t * tile_rows
-        spread = nn(ones_where((index >> 4) == iota((tile_rows, shards), 1)), heads)
-        index = iota((tile_rows, LANES), 0) + t * tile_rows
-        mine = jnp.where(((index >> 2) & 3) == iota((tile_rows, LANES), 1), spread, 0.0)
+    span = column * BLOCK
+
+    def answer(step):
+        away = (step + 1) >> 1
+        off = jnp.where((step & 1) == 1, away, nz - away)
+        z_from = lax.rem(z + off, nz)
+        first = z_from * column
+
+        @pl.when(step == 0)
+        def _():
+            pltpu.make_async_copy(
+                head_recv.at[pl.ds(0, column - 1)], head_recv.at[pl.ds(0, column - 1)], head_sems.at[0]).wait()
+
+        @pl.when(step > 0)
+        def _():
+            whole = head_recv.at[pl.ds(0, column)]
+            pltpu.make_async_copy(whole, whole, head_sems.at[lax.rem(off, nz)]).wait()
+
+        heads = head_recv[pl.ds(first, column)].reshape(column, LANES).astype(BF16)
+        spread = nn(ones_where((iota((span, column), 0) >> 4) == iota((span, column), 1)), heads)
+        index = iota((span, LANES), 0)
+        mine = jnp.where(((index >> 2) & 3) == iota((span, LANES), 1), spread, 0.0)
         asked = jnp.sum(mine, axis=1, keepdims=True).astype(jnp.int32) - 1
         quarter = index[:, 0:1] & 3
-        out = jnp.zeros((tile_rows, width), F32)
+        out = jnp.zeros((span, width), F32)
         for q in range(QUARTERS):
             key = jnp.where(quarter == q, asked, -1)
-            pick = ones_where(key == iota((tile_rows, slots), 1))
+            pick = ones_where(key == iota((span, slots), 1))
             out = out + nn(pick, table_ref[:, q * width:(q + 1) * width])
-        rows_send[block(t, tile_rows), :] = out.astype(BF16)
-    loop(0, rows // tile_rows, answer)
-
-    def send_rows(k):
-        p = lax.rem(s + k, shards)
-        copy(3, rows_send.at[block(p, BLOCK)], rows_recv.at[block(s, BLOCK)], (g, p)).start()
-    loop(1, shards, send_rows)
+        rows_send[block(z_from, span), :] = out.astype(BF16)
+
+        def send_rows(k):
+            p = first + k
+
+            @pl.when(p != s)
+            def _():
+                copy(3, rows_send.at[block(p, BLOCK)], rows_recv.at[block(s, BLOCK)], (g, p)).start()
+        loop(0, column, send_rows)
+    loop(0, nz, answer)
     rows_recv[block(s, BLOCK), :] = rows_send[block(s, BLOCK), :]
 
     others = pl.ds(0, half - BLOCK)
@@ -187,6 +226,7 @@
     mine = pl.ds(pl.multiple_of(core * half, half), half)
     copy(4, users_all.at[mine], users_all.at[mine], partner).start()
 
+    heads = head_recv[...].reshape(shards, LANES).astype(BF16)
     held = tn(heads, ones_where((iota((shards, rows), 1) >> 4) == iota((shards, rows), 0)))
     lane = iota((LANES, rows), 1)
     held = jnp.where(((lane >> 2) & 3) == iota((LANES, rows), 0), held, 0.0)
@@ -198,9 +238,10 @@
         where = c_u * chips + (chip_u & (nx - 1)) * nz + (chip_u >> (nx.bit_length() - 1))
         return (where * CAP + user) * QUARTERS
 
-    key_rows = [user_key(ids_ref[2 + side:3 + side, :]) for side in range(2)]
+    key_rows = [user_key(pair_ref[side:side + 1, :]) for side in range(2)]
     key_cols = [as_column(row) for row in key_rows]
-    expand = ones_where(iota((LANES, width), 0) == (iota((LANES, width), 1) >> 4))
+    gate = iota((LANES, width), 0)
+    expand = ones_where((gate < COMPS * COMPS) & ((gate & 15) == (iota((LANES, width), 1) >> 4)))
     wait_recv(4, users_all.at[mine])
     for side in range(2):
         def pick_users(q):
@@ -233,6 +274,11 @@
     pairs = COMPS * GROUP
 
     def pair_loss(b):
+        stores = []
+
+        def store(ref, where, lanes, values):
+            stores.append((ref, where, lanes, values))
+
         comb = stack(combined, b, 1)
         scale = lax.rsqrt(jnp.mean(comb * comb, axis=1, keepdims=True) + 1e-06)
         normed = comb * scale
@@ -262,19 +308,27 @@
         d_row = d_row.astype(BF16)
         for p in range(COMPS):
             part = d_row[p * GROUP:(p + 1) * GROUP]
-            d_comb[spot(p >> 1, b), lanes_of(p)] = part
+            store(d_comb, spot(p >> 1, b), lanes_of(p), part)
             item, column = block(b, GROUP), slice(p * LANES, (p + 1) * LANES)
-            d_pre[item, column] = (part.astype(F32) * slope[item, column]).astype(BF16)
+            store(d_pre, item, column, (part.astype(F32) * slope[item, column]).astype(BF16))
         for side in range(2):
             for p in range(COMPS):
                 here = spot(side * QUARTERS + (p >> 1), b)
                 part = slice(side * pairs + p * GROUP, side * pairs + (p + 1) * GROUP)
                 lane0 = (p & 1) * LANES
-                d_users[here, lane0:lane0 + LANES] = du_high[part]
-                d_users[here, width + lane0:width + lane0 + LANES] = du_low[part]
-                d_gates[here, lane0:lane0 + LANES] = dg_high[part]
-                d_gates[here, width + lane0:width + lane0 + LANES] = dg_low[part]
-    loop(0, n // GROUP, pair_loss)
+                store(d_users, here, slice(lane0, lane0 + LANES), du_high[part])
+                store(d_users, here, slice(width + lane0, width + lane0 + LANES), du_low[part])
+                store(d_gates, here, slice(lane0, lane0 + LANES), dg_high[part])
+                store(d_gates, here, slice(width + lane0, width + lane0 + LANES), dg_low[part])
+        return stores
+
+    together = 2 - (n // GROUP) % 2
+
+    def pair_losses(t):
+        for stores in [pair_loss(t * together + i) for i in range(together)]:
+            for ref, where, lanes, values in stores:
+                ref[where, lanes] = values
+    loop(0, n // (GROUP * together), pair_losses)
 
     copy(5, d_pre, d_pre_recv, partner).start()
 
@@ -284,32 +338,34 @@
         back_send[block(t, tile_rows), :] = nn(put, d_comb[...]).astype(BF16)
     loop(0, rows // tile_rows, give_back)
 
+    wait_recv(2, xt_recv)
+    wait_recv(5, d_pre_recv)
+    wide = nz * depth
+
+    def tower_rows(i):
+        here = block(i, wide)
+        total = nn(xt[core, here, :], d_pre[...]) + nn(xt_recv[here, :], d_pre_recv[...])
+        tower_part[here, :] = total.astype(BF16)
+    loop(0, nx, tower_rows)
+
+    def send_x(k):
+        to = lax.rem(x + k, nx)
+        copy(8, tower_part.at[block(to, wide)], tower_x.at[x], at(z, to, core)).start()
+    loop(1, nx, send_x)
+
     def send_back(k):
         p = lax.rem(s + k, shards)
         copy(6, back_send.at[block(p, BLOCK)], back_recv.at[block(s, BLOCK)], (g, p)).start()
     loop(1, shards, send_back)
     back_recv[block(s, BLOCK), :] = back_send[block(s, BLOCK), :]
 
-    wait_recv(2, xt_recv)
-    wait_recv(5, d_pre_recv)
-    wide = nz * depth
-
-    def tower_rows(i):
-        here = block(i, wide)
-        total = nn(xt[core, here, :], d_pre[...]) + nn(xt_recv[here, :], d_pre_recv[...])
-        tower_part[here, :] = total.astype(BF16)
-    loop(0, nx, tower_rows)
-
-    def send_x(k):
-        to = lax.rem(x + k, nx)
-        copy(8, tower_part.at[block(to, wide)], tower_x.at[x], at(z, to, core)).start()
-    loop(1, nx, send_x)
-
     def squeeze(i):
         here = block(i, n)
         high, low = halves(nt(d_gates[here, :width], expand) + nt(d_gates[here, width:], expand))
-        d_users[here, 2 * width:2 * width + LANES] = high
-        d_users[here, 2 * width + LANES:] = low
+        ours = (iota((n, LANES), 1) >> 4) == (i & 3)
+        zero = jnp.zeros((n, LANES), BF16)
+        d_users[here, 2 * width:2 * width + LANES] = jnp.where(ours, high, zero)
+        d_users[here, 2 * width + LANES:] = jnp.where(ours, low, zero)
     loop(0, 2 * QUARTERS, squeeze)
 
     tile_users = min(128, rows)
@@ -377,8 +433,14 @@
     total = users_mid[block(z, BLOCK), :].astype(F32)
     for k in range(1, nz):
         total = total + users_z[lax.rem(z + k, nz)].astype(F32)
-    users_out[...] = total[:, :width]
-    gates_out[...] = total[:, width:]
+    own_rows[...] = total
+    for u in range(CAP):
+        gate_row = jnp.zeros((1, COMPS * COMPS), F32)
+        for q in range(QUARTERS):
+            row = u * QUARTERS + q
+            users_out[u:u + 1, q * width:(q + 1) * width] = own_rows[row:row + 1, :width]
+            gate_row = gate_row + own_rows[row:row + 1, width:width + COMPS * COMPS]
+        gates_out[u:u + 1, :] = gate_row
 
     tower_y[g] = tower_low[...]
     wait_recv(12, tower_y.at[pl.ds(0, groups - 1)])
@@ -414,12 +476,8 @@
     half = rows // CORES
     depth = d // shards
     across = width + LANES
-    ids = jnp.concatenate(
-        [owner.reshape(1, n), table_slot.reshape(1, n), pair_users.T], axis=0)
-    gates = user_gates.reshape(held * QUARTERS, -1)
-    own_users = jnp.concatenate(
-        [user_comps.reshape(BLOCK, width), jnp.pad(gates, ((0, 0), (0, LANES - gates.shape[1])))], axis=1)
     scratch = [
+        ((d, d), BF16), ((BLOCK, across), F32), ((BLOCK, across), BF16),
         ((shards, 1, LANES), F32), ((shards, 1, LANES), F32),
         ((rows, across), BF16),
         ((CORES, d // 2, n), BF16), ((d // 2, n), BF16),
@@ -437,24 +495,23 @@
         ((rows, width), BF16), ((rows, width), BF16),
     ]
     whole = pl.BlockSpec(memory_space=pltpu.VMEM)
-    tower_grad, table_grad, user_rows, gate_rows = pl.pallas_call(
+    return pl.pallas_call(
         functools.partial(kernel, groups, shards, nx),
         out_shape=(
             jax.ShapeDtypeStruct((depth, d), F32),
             jax.ShapeDtypeStruct((slots, d), F32),
-            jax.ShapeDtypeStruct((BLOCK, width), F32),
-            jax.ShapeDtypeStruct((BLOCK, LANES), F32),
+            jax.ShapeDtypeStruct((held, d), F32),
+            jax.ShapeDtypeStruct((held, COMPS * COMPS), F32),
         ),
-        in_specs=[whole] * 5,
+        in_specs=[whole] * 4 + [pl.BlockSpec(memory_space=pltpu.HBM)] + [whole] * 3,
         out_specs=(whole,) * 4,
         scratch_shapes=[pltpu.VMEM(shape, kind) for shape, kind in scratch]
-        + [pltpu.SemaphoreType.DMA((13,)), pltpu.SemaphoreType.DMA((13,))],
+        + [pltpu.SemaphoreType.DMA((13,)), pltpu.SemaphoreType.DMA((13,)), pltpu.SemaphoreType.DMA((nz,)),
+           pltpu.SemaphoreType.DMA],
         compiler_params=pltpu.CompilerParams(
-            collective_id=0, has_side_effects=True, vmem_limit_bytes=56 * 1024 * 1024),
-    )(ids, item_features, tower_weight, item_table, own_users)
-    user_comp_grad = user_rows.reshape(held, d)
-    user_gate_grad = gate_rows[:, : gates.shape[1]].reshape(held, -1)
-    return tower_grad, table_grad, user_comp_grad, user_gate_grad
+            collective_id=0, has_side_effects=True, vmem_limit_bytes=32 * 1024 * 1024),
+    )(owner.reshape(1, n), table_slot.reshape(1, n), pair_users.T, item_features, tower_weight, item_table,
+      user_comps, user_gates)
 
 
 def solution(mesh):

time: 99.2 us -> 95.6 us (0.964)
  the two profiles are of different devices: /device:TPU:2 before, /device:TPU:128 now
where the time goes in v1:
time: 95.6 us; the launch traced here: 95.3 us
  Pallas kernels  85.2 us (89%)
  local copies, waits for them, and re-layouts  9.45 us (10%)
    pallas_call x1, Pallas kernels, local(): pl.pallas_call(functools.partial(kernel, groups, shards, nx), out_shape=(...  85.2 us
    unnamed x20, local copies, waits for them, and re-layouts  9.45 us

profile of v1, /device:TPU:128, one launch (start us, length us, event | category | flops | bytes accessed | tf_op | source)
XLA Modules:
  0.0 95.3 jit_solution(7994338377908877819)
XLA Ops:
  0.6 0.0 copy-start
  0.6 1.6 %copy-done = bf16[1024,1024]{1,0:T(8,128)(2,1)S(1)} copy-done((bf16[1024,1024]{1,0:T(8,128)(2,1)S(1)}, bf16[1024,1024]{1,0:T(8,128)(2,1)}, u32[]{:S(2)}) %copy-start) | copy-done | bytes 2097176
  2.2 0.0 copy-start.1
  2.2 0.9 copy-done.1
  3.2 0.0 copy-start.2
  3.2 0.9 copy-done.2
  4.1 0.0 copy-start.3
  4.1 0.7 copy-done.3
  4.8 0.0 copy-start.4
  4.8 0.7 copy-done.4
  5.5 0.0 copy-start.5
  5.5 0.7 copy-done.5
  6.2 0.0 copy-start.6
  6.2 0.7 copy-done.6
  6.8 0.0 copy-start.7
  6.8 0.7 copy-done.7
  7.5 85.2 %shard_map.111 = (f32[16,1024]{1,0:T(8,128)S(1)}, f32[128,1024]{1,0:T(8,128)S(1)}, f32[4,1024]{1,0:T(4,128)S(1)}, f32[4,64]{1,0:T(4,128)S(1)}) custom-call(s32[1,128]{1,0:T(1,128)S(1)} %bitcast.4, s32[1,128]{1,0:T(1,128)S(1)} %bitcast.5, s32[2,128]{1,0:T(2,128)S(1)} %bitcast.3, bf16[128,1024]{1,0:T(8,128)(2,1)S(1)} %copy-done.1, ...), custom_call_target="tpu_custom_call" | custom-call | tf_op jit(solution)/shard_map/pallas_call | solution.py:498
  92.7 0.6 copy.16
  93.4 0.8 copy.17
  94.2 0.6 copy.18
  94.8 0.6 copy.19
Async XLA Ops:
  0.6 1.6 %copy-start = (bf16[1024,1024]{1,0:T(8,128)(2,1)S(1)}, bf16[1024,1024]{1,0:T(8,128)(2,1)}, u32[]{:S(2)}) copy-start(bf16[1024,1024]{1,0:T(8,128)(2,1)} %w_hbm.1) | copy-start | bytes 6291460
  2.2 0.9 copy-start.1
  3.2 0.9 copy-start.2
  4.1 0.7 copy-start.3
  4.8 0.7 copy-start.4
  5.5 0.7 copy-start.5
  6.2 0.7 copy-start.6
  6.8 0.7 copy-start.7

commit v2 on v1

--- a/solution.py
+++ b/solution.py
@@ -54,6 +54,7 @@
     w_ref, own_rows, own_users, head_send, head_recv, users_all, xt, xt_recv, embedded, slope, rows_send, rows_recv,
     picked, gates_wide, combined, d_comb, d_pre, d_pre_recv, d_users, d_gates,
     users_part, users_part_recv, tower_part, tower_x, tower_mid, tower_z, tower_low, tower_y,
+    other_part, other_y, other_mid, other_x, other_low, other_z, other_got,
     users_half, users_x, users_mid, users_z, back_send, back_recv,
     send_sems, recv_sems, head_sems, w_sem,
 ):
@@ -338,6 +339,8 @@
         back_send[block(t, tile_rows), :] = nn(put, d_comb[...]).astype(BF16)
     loop(0, rows // tile_rows, give_back)
 
+    first = tower_part.shape[1]
+    deep = nx * depth
     wait_recv(2, xt_recv)
     wait_recv(5, d_pre_recv)
     wide = nz * depth
@@ -345,13 +348,21 @@
     def tower_rows(i):
         here = block(i, wide)
         total = nn(xt[core, here, :], d_pre[...]) + nn(xt_recv[here, :], d_pre_recv[...])
-        tower_part[here, :] = total.astype(BF16)
+        tower_part[here, :] = total[:, :first].astype(BF16)
+        for j in range(nz):
+            there = pl.ds(pl.multiple_of((j * nx + i) * depth, depth), depth)
+            other_part[there, :] = total[j * depth:(j + 1) * depth, first:].astype(BF16)
     loop(0, nx, tower_rows)
 
     def send_x(k):
         to = lax.rem(x + k, nx)
         copy(8, tower_part.at[block(to, wide)], tower_x.at[x], at(z, to, core)).start()
     loop(1, nx, send_x)
+
+    def send_other_y(k):
+        to = lax.rem(g + k, groups)
+        copy(13, other_part.at[block(to, deep)], other_y.at[g], (to, s)).start()
+    loop(1, groups, send_other_y)
 
     def send_back(k):
         p = lax.rem(s + k, shards)
@@ -401,6 +412,17 @@
         copy(10, tower_mid.at[block(to, depth)], tower_z.at[z], at(to, x, core)).start()
     loop(1, nz, send_z)
 
+    wait_recv(13, other_y.at[pl.ds(0, groups - 1)])
+    total = other_part[block(g, deep), :].astype(F32)
+    for k in range(1, groups):
+        total = total + other_y[lax.rem(g + k, groups)].astype(F32)
+    other_mid[...] = total.astype(BF16)
+
+    def send_other_x(k):
+        to = lax.rem(x + k, nx)
+        copy(14, other_mid.at[block(to, depth)], other_x.at[x], at(z, to, core)).start()
+    loop(1, nx, send_other_x)
+
     wait_recv(9, users_x.at[pl.ds(0, nx - 1)])
     total = users_half[block(x, tall), :].astype(F32)
     for k in range(1, nx):
@@ -411,6 +433,38 @@
         to = lax.rem(z + k, nz)
         copy(11, users_mid.at[block(to, BLOCK)], users_z.at[z], at(to, x, core)).start()
     loop(1, nz, send_uz)
+
+    wait_recv(14, other_x.at[pl.ds(0, nx - 1)])
+    total = other_mid[block(x, depth), :].astype(F32)
+    for k in range(1, nx):
+        total = total + other_x[lax.rem(x + k, nx)].astype(F32)
+    other_low[...] = total
+
+    @pl.when(z != g)
+    def _():
+        copy(15, other_low, other_z.at[z], at(g, x, core)).start()
+
+    wait_recv(10, tower_z.at[pl.ds(0, nz - 1)])
+    total = tower_mid[block(z, depth), :].astype(F32)
+    for k in range(1, nz):
+        total = total + tower_z[lax.rem(z + k, nz)].astype(F32)
+    tower_low[...] = total.astype(BF16)
+
+    def send_y(k):
+        copy(12, tower_low, tower_y.at[g], (lax.rem(g + k, groups), s)).start()
+    loop(1, groups, send_y)
+
+    @pl.when(z == g)
+    def _():
+        wait_recv(15, other_z.at[pl.ds(0, nz - 1)])
+        total = other_low[...]
+        for k in range(1, nz):
+            total = total + other_z[lax.rem(z + k, nz)]
+        other_got[...] = total.astype(BF16)
+
+        def send_other(k):
+            copy(16, other_got, other_got, (lax.rem(g + k, groups), s)).start()
+        loop(1, groups, send_other)
 
     wait_recv(6, back_recv.at[pl.ds(0, rows - BLOCK)])
     quarter_row = iota((1, rows), 1) & 3
@@ -418,16 +472,6 @@
         key = jnp.where(quarter_row == q, asked_row, -1)
         pick = ones_where(key == iota((slots, rows), 0))
         table_out[:, q * width:(q + 1) * width] = nn(pick, back_recv[...])
-
-    wait_recv(10, tower_z.at[pl.ds(0, nz - 1)])
-    total = tower_mid[block(z, depth), :].astype(F32)
-    for k in range(1, nz):
-        total = total + tower_z[lax.rem(z + k, nz)].astype(F32)
-    tower_low[...] = total.astype(BF16)
-
-    def send_y(k):
-        copy(12, tower_low, tower_y.at[g], (lax.rem(g + k, groups), s)).start()
-    loop(1, groups, send_y)
 
     wait_recv(11, users_z.at[pl.ds(0, nz - 1)])
     total = users_mid[block(z, BLOCK), :].astype(F32)
@@ -447,7 +491,20 @@
     total = tower_y[0].astype(F32)
     for k in range(1, groups):
         total = total + tower_y[k].astype(F32)
-    tower_out[...] = total
+    tower_out[:, :first] = total
+
+    @pl.when(z != g)
+    def _():
+        wait_recv(16, other_got)
+        wait_send(15, other_low)
+
+    @pl.when(z == g)
+    def _():
+        wait_send(16, other_part.at[pl.ds(0, (groups - 1) * depth)])
+
+    tower_out[:, first:] = other_got[...].astype(F32)
+    wait_send(13, other_y.at[pl.ds(0, groups - 1)])
+    wait_send(14, other_x.at[pl.ds(0, nx - 1)])
 
     wait_send(0, head_send.at[pl.ds(0, shards - 1)])
     wait_send(1, users_all.at[others])
@@ -476,6 +533,9 @@
     half = rows // CORES
     depth = d // shards
     across = width + LANES
+    first = d * 5 // 8
+    other = d - first
+    assert groups == nz
     scratch = [
         ((d, d), BF16), ((BLOCK, across), F32), ((BLOCK, across), BF16),
         ((shards, 1, LANES), F32), ((shards, 1, LANES), F32),
@@ -488,8 +548,10 @@
         ((n, d), BF16), ((n, d), BF16),
         ((2 * QUARTERS * n, 2 * across), BF16), ((2 * QUARTERS * n, 2 * width), BF16),
         ((rows, across), F32), ((half, across), F32),
-        ((d // 2, d), BF16), ((nx, nz * depth, d), BF16), ((nz * depth, d), BF16),
-        ((nz, depth, d), BF16), ((depth, d), BF16), ((groups, depth, d), BF16),
+        ((d // 2, first), BF16), ((nx, nz * depth, first), BF16), ((nz * depth, first), BF16),
+        ((nz, depth, first), BF16), ((depth, first), BF16), ((groups, depth, first), BF16),
+        ((d // 2, other), BF16), ((groups, nx * depth, other), BF16), ((nx * depth, other), BF16),
+        ((nx, depth, other), BF16), ((depth, other), F32), ((nz, depth, other), F32), ((depth, other), BF16),
         ((half, across), BF16), ((nx, nz * BLOCK, across), BF16), ((nz * BLOCK, across), BF16),
         ((nz, BLOCK, across), BF16),
         ((rows, width), BF16), ((rows, width), BF16),
@@ -506,12 +568,13 @@
         in_specs=[whole] * 4 + [pl.BlockSpec(memory_space=pltpu.HBM)] + [whole] * 3,
         out_specs=(whole,) * 4,
         scratch_shapes=[pltpu.VMEM(shape, kind) for shape, kind in scratch]
-        + [pltpu.SemaphoreType.DMA((13,)), pltpu.SemaphoreType.DMA((13,)), pltpu.SemaphoreType.DMA((nz,)),
+        + [pltpu.SemaphoreType.DMA((17,)), pltpu.SemaphoreType.DMA((17,)), pltpu.SemaphoreType.DMA((nz,)),
            pltpu.SemaphoreType.DMA],
         compiler_params=pltpu.CompilerParams(
             collective_id=0, has_side_effects=True, vmem_limit_bytes=32 * 1024 * 1024),
-    )(owner.reshape(1, n), table_slot.reshape(1, n), pair_users.T, item_features, tower_weight, item_table,
-      user_comps, user_gates)
+    )(*(pltpu.with_memory_space_constraint(a, pltpu.HBM) for a in (
+        owner.reshape(1, n), table_slot.reshape(1, n), pair_users.T, item_features, tower_weight, item_table,
+        user_comps, user_gates)))
 
 
 def solution(mesh):

time: 95.6 us -> 80 us (0.84)
  the two profiles are of different devices: /device:TPU:128 before, /device:TPU:32 now
where the time goes in v2:
time: 80 us; the launch traced here: 79.9 us
  Pallas kernels  76.6 us (96%)
  local copies, waits for them, and re-layouts  2.61 us (3%)
    pallas_call x1, Pallas kernels, local(): pl.pallas_call(functools.partial(kernel, groups, shards, nx), out_shape=(...  76.6 us
    unnamed x4, local copies, waits for them, and re-layouts  2.61 us

profile of v2, /device:TPU:32, one launch (start us, length us, event | category | flops | bytes accessed | tf_op | source)
XLA Modules:
  0.0 79.9 jit_solution(8091862122488865322)
XLA Ops:
  0.6 76.6 %shard_map.111 = (f32[16,1024]{1,0:T(8,128)S(1)}, f32[128,1024]{1,0:T(8,128)S(1)}, f32[4,1024]{1,0:T(4,128)S(1)}, f32[4,64]{1,0:T(4,128)S(1)}) custom-call(s32[1,128]{1,0:T(1,128)} %bitcast.4, s32[1,128]{1,0:T(1,128)} %bitcast.5, s32[2,128]{1,0:T(2,128)} %bitcast.3, bf16[128,1024]{1,0:T(8,128)(2,1)} %x_ref.1, bf16[1024,1024]{1,0:T(8,128)(2,1)} %w_hbm.1, ...), custom_call_target="tpu_custom_call" | custom-call | tf_op jit(solution)/shard_map/pallas_call | solution.py:560
  77.3 0.6 copy.16
  77.9 0.8 copy.17
  78.7 0.6 copy.18
  79.3 0.6 copy.19

commit v3 on v2

--- a/solution.py
+++ b/solution.py
@@ -49,14 +49,15 @@
 
 def kernel(
     groups, shards, nx,
-    owner_ref, slot_ref, pair_ref, x_ref, w_hbm, table_ref, comps_ref, gates_ref,
+    owner_hbm, slot_hbm, pair_hbm, comps_hbm, gates_hbm, x_hbm, w_hbm, table_hbm,
     tower_out, table_out, users_out, gates_out,
-    w_ref, own_rows, own_users, head_send, head_recv, users_all, xt, xt_recv, embedded, slope, rows_send, rows_recv,
+    owner_ref, slot_ref, pair_ref, comps_ref, gates_ref, x_ref, w_ref, table_ref,
+    own_rows, own_users, own_gates, gates_all, head_send, head_recv, users_all, xt, xt_recv, embedded, slope, rows_send, rows_recv,
     picked, gates_wide, combined, d_comb, d_pre, d_pre_recv, d_users, d_gates,
     users_part, users_part_recv, tower_part, tower_x, tower_mid, tower_z, tower_low, tower_y,
     other_part, other_y, other_mid, other_x, other_low, other_z, other_got,
     users_half, users_x, users_mid, users_z, back_send, back_recv,
-    send_sems, recv_sems, head_sems, w_sem,
+    send_sems, recv_sems, head_sems, load_sems,
 ):
     n, d = x_ref.shape
     slots = table_ref.shape[0]
@@ -98,13 +99,22 @@
     def block(i, size):
         return pl.ds(pl.multiple_of(i * size, size), size)
 
-    load_w = pltpu.make_async_copy(w_hbm, w_ref, w_sem)
-    load_w.start()
+    loads = [
+        pltpu.make_async_copy(source, target, load_sems.at[i])
+        for i, (source, target) in enumerate((
+            (owner_hbm, owner_ref), (slot_hbm, slot_ref), (pair_hbm, pair_ref), (comps_hbm, comps_ref),
+            (gates_hbm, gates_ref), (x_hbm, x_ref), (w_hbm, w_ref), (table_hbm, table_ref)))
+    ]
+    for load in loads:
+        load.start()
     barrier = pltpu.get_barrier_semaphore()
     loop(1, shards, lambda k: pl.semaphore_signal(
         barrier, inc=1, device_id=(g, lax.rem(s + k, shards)), device_id_type=MESH))
     loop(1, groups, lambda k: pl.semaphore_signal(
         barrier, inc=1, device_id=(lax.rem(g + k, groups), s), device_id_type=MESH))
+
+    for load in loads[:5]:
+        load.wait()
 
     target = owner_ref[...]
     slot = slot_ref[...]
@@ -124,18 +134,18 @@
     turn = ones_where(iota((LANES, n), 0) == within)
     head_send[...] = nt(wanted, turn).reshape(shards, 1, LANES)
 
-    own_rows[:, width:] = jnp.zeros((BLOCK, LANES), F32)
-    gate_lane = iota((1, COMPS * COMPS), 1)
-    own_comps, own_gates = comps_ref[...].astype(F32), gates_ref[...].astype(F32)
+    own_comps, gate_values = comps_ref[...].astype(F32), gates_ref[...].astype(F32)
     for u in range(CAP):
         for q in range(QUARTERS):
             row = u * QUARTERS + q
             own_rows[row:row + 1, :width] = own_comps[u:u + 1, q * width:(q + 1) * width]
-            own_rows[row:row + 1, width:width + COMPS * COMPS] = jnp.where(
-                (gate_lane >> 4) == q, own_gates[u:u + 1, :], 0.0)
-    own_users[...] = own_rows[...].astype(BF16)
+    own_users[...] = own_rows[:, :width].astype(BF16)
+    for pair in range(CAP // 2):
+        own_gates[pair] = jnp.concatenate([gate_values[2 * pair:2 * pair + 1], gate_values[2 * pair + 1:2 * pair + 2]], axis=1)
     own = core * chips + x * nz + z
     users_all[block(own, BLOCK), :] = own_users[...]
+    gate_rows = CAP // 2
+    gates_all[pl.ds(own * gate_rows, gate_rows)] = own_gates[...]
 
     pl.semaphore_wait(barrier, shards - 1 + groups - 1)
 
@@ -157,7 +167,10 @@
     def send_users(k):
         p = lax.rem(chip + k, chips)
         copy(1, own_users, users_all.at[block(own, BLOCK)], (g, p * CORES + core)).start()
+        copy(17, own_gates, gates_all.at[pl.ds(own * gate_rows, gate_rows)], (g, p * CORES + core)).start()
     loop(1, chips, send_users)
+    loads[5].wait()
+
     for tile in range(d // LANES):
         turned = x_ref[:, tile * LANES:(tile + 1) * LANES].astype(F32).T.astype(BF16)
         for piece in range(max(1, LANES // depth)):
@@ -170,7 +183,7 @@
 
     copy(2, xt.at[1 - core], xt_recv, partner).start()
 
-    load_w.wait()
+    loads[6].wait()
 
     def tower(q):
         columns = block(q, width)
@@ -219,6 +232,7 @@
             def _():
                 copy(3, rows_send.at[block(p, BLOCK)], rows_recv.at[block(s, BLOCK)], (g, p)).start()
         loop(0, column, send_rows)
+    loads[7].wait()
     loop(0, nz, answer)
     rows_recv[block(s, BLOCK), :] = rows_send[block(s, BLOCK), :]
 
@@ -226,6 +240,10 @@
     wait_recv(1, users_all.at[others])
     mine = pl.ds(pl.multiple_of(core * half, half), half)
     copy(4, users_all.at[mine], users_all.at[mine], partner).start()
+    other_gates = pl.ds(0, (chips - 1) * gate_rows)
+    wait_recv(17, gates_all.at[other_gates])
+    my_gates = pl.ds(core * chips * gate_rows, chips * gate_rows)
+    copy(18, gates_all.at[my_gates], gates_all.at[my_gates], partner).start()
 
     heads = head_recv[...].reshape(shards, LANES).astype(BF16)
     held = tn(heads, ones_where((iota((shards, rows), 1) >> 4) == iota((shards, rows), 0)))
@@ -244,13 +262,21 @@
     gate = iota((LANES, width), 0)
     expand = ones_where((gate < COMPS * COMPS) & ((gate & 15) == (iota((LANES, width), 1) >> 4)))
     wait_recv(4, users_all.at[mine])
+    wait_recv(18, gates_all.at[my_gates])
+    gate_table = gates_all[...].reshape(shards * gate_rows, LANES).astype(BF16)
+    gate_lane = iota((LANES, width), 0)
+    gate_of = (gate_lane & 15) == (iota((LANES, width), 1) >> 4)
     for side in range(2):
+        user = key_cols[side] >> 2
+        taken = nn(ones_where((user >> 1) == iota((n, shards * gate_rows), 1)), gate_table)
+        taken = jnp.where((iota((n, LANES), 1) >> 6) == (user & 1), taken, 0.0).astype(BF16)
+
         def pick_users(q):
             pick = ones_where(key_cols[side] + q == iota((n, rows), 1))
-            got = nn(pick, users_all[...]).astype(BF16)
             here = block(side * QUARTERS + q, n)
-            picked[here, :] = got[:, :width]
-            gates_wide[here, :] = nn(got[:, width:], expand).astype(BF16)
+            picked[here, :] = nn(pick, users_all[...]).astype(BF16)
+            part = ones_where(gate_of & (((gate_lane & 63) >> 4) == q))
+            gates_wide[here, :] = nn(taken, part).astype(BF16)
         loop(0, QUARTERS, pick_users)
 
     wait_recv(3, rows_recv.at[pl.ds(0, rows - BLOCK)])
@@ -364,10 +390,20 @@
         copy(13, other_part.at[block(to, deep)], other_y.at[g], (to, s)).start()
     loop(1, groups, send_other_y)
 
-    def send_back(k):
-        p = lax.rem(s + k, shards)
-        copy(6, back_send.at[block(p, BLOCK)], back_recv.at[block(s, BLOCK)], (g, p)).start()
-    loop(1, shards, send_back)
+    far = max(1, 3 * nz // 8)
+
+    def send_back(step):
+        away = (step + 1) >> 1
+        z_to = lax.rem(z + nz // 2 + jnp.where((step & 1) == 1, nz - away, away), nz)
+
+        def send_one(k):
+            p = z_to * column + k
+
+            @pl.when(p != s)
+            def _():
+                copy(6, back_send.at[block(p, BLOCK)], back_recv.at[block(s, BLOCK)], (g, p)).start()
+        loop(0, column, send_one)
+    loop(0, far, send_back)
     back_recv[block(s, BLOCK), :] = back_send[block(s, BLOCK), :]
 
     def squeeze(i):
@@ -411,6 +447,7 @@
         to = lax.rem(z + k, nz)
         copy(10, tower_mid.at[block(to, depth)], tower_z.at[z], at(to, x, core)).start()
     loop(1, nz, send_z)
+    loop(far, nz, send_back)
 
     wait_recv(13, other_y.at[pl.ds(0, groups - 1)])
     total = other_part[block(g, deep), :].astype(F32)
@@ -508,6 +545,8 @@
 
     wait_send(0, head_send.at[pl.ds(0, shards - 1)])
     wait_send(1, users_all.at[others])
+    wait_send(17, gates_all.at[other_gates])
+    wait_send(18, gates_all.at[my_gates])
     wait_send(2, xt_recv)
     wait_send(3, rows_send.at[pl.ds(0, rows - BLOCK)])
     wait_send(4, users_all.at[mine])
@@ -537,9 +576,11 @@
     other = d - first
     assert groups == nz
     scratch = [
-        ((d, d), BF16), ((BLOCK, across), F32), ((BLOCK, across), BF16),
+        ((1, n), jnp.int32), ((1, n), jnp.int32), ((2, n), jnp.int32), ((held, d), BF16), ((held, COMPS * COMPS), BF16),
+        ((n, d), BF16), ((d, d), BF16), ((slots, d), BF16),
+        ((BLOCK, across), F32), ((BLOCK, width), BF16), ((CAP // 2, 1, LANES), F32), ((shards * CAP // 2, 1, LANES), F32),
         ((shards, 1, LANES), F32), ((shards, 1, LANES), F32),
-        ((rows, across), BF16),
+        ((rows, width), BF16),
         ((CORES, d // 2, n), BF16), ((d // 2, n), BF16),
         ((QUARTERS * n, width), BF16), ((n, d), F32),
         ((rows, width), BF16), ((rows, width), BF16),
@@ -565,16 +606,16 @@
             jax.ShapeDtypeStruct((held, d), F32),
             jax.ShapeDtypeStruct((held, COMPS * COMPS), F32),
         ),
-        in_specs=[whole] * 4 + [pl.BlockSpec(memory_space=pltpu.HBM)] + [whole] * 3,
+        in_specs=[pl.BlockSpec(memory_space=pltpu.HBM)] * 8,
         out_specs=(whole,) * 4,
         scratch_shapes=[pltpu.VMEM(shape, kind) for shape, kind in scratch]
-        + [pltpu.SemaphoreType.DMA((17,)), pltpu.SemaphoreType.DMA((17,)), pltpu.SemaphoreType.DMA((nz,)),
-           pltpu.SemaphoreType.DMA],
+        + [pltpu.SemaphoreType.DMA((19,)), pltpu.SemaphoreType.DMA((19,)), pltpu.SemaphoreType.DMA((nz,)),
+           pltpu.SemaphoreType.DMA((8,))],
         compiler_params=pltpu.CompilerParams(
             collective_id=0, has_side_effects=True, vmem_limit_bytes=32 * 1024 * 1024),
     )(*(pltpu.with_memory_space_constraint(a, pltpu.HBM) for a in (
-        owner.reshape(1, n), table_slot.reshape(1, n), pair_users.T, item_features, tower_weight, item_table,
-        user_comps, user_gates)))
+        owner.reshape(1, n), table_slot.reshape(1, n), pair_users.T, user_comps, user_gates,
+        item_features, tower_weight, item_table)))
 
 
 def solution(mesh):

time: 80 us -> 77.1 us (0.964)
  Pallas kernels: 76.6 us -> 73.8 us
    pallas_call x1, Pallas kernels: 76.6 us -> 73.8 us  [local(): pl.pallas_call(functools.partial(kernel, groups, shards, nx), out_shape=(...]
where the time goes in v3:
time: 77.1 us; the launch traced here: 77 us
  Pallas kernels  73.8 us (96%)
  local copies, waits for them, and re-layouts  2.61 us (3%)
    pallas_call x1, Pallas kernels, local(): pl.pallas_call(functools.partial(kernel, groups, shards, nx), out_shape=(...  73.8 us
    unnamed x4, local copies, waits for them, and re-layouts  2.61 us

profile of v3, /device:TPU:32, one launch (start us, length us, event | category | flops | bytes accessed | tf_op | source)
XLA Modules:
  0.0 77.0 jit_solution(6505337235355841523)
XLA Ops:
  0.6 73.8 %shard_map.111 = (f32[16,1024]{1,0:T(8,128)S(1)}, f32[128,1024]{1,0:T(8,128)S(1)}, f32[4,1024]{1,0:T(4,128)S(1)}, f32[4,64]{1,0:T(4,128)S(1)}) custom-call(s32[1,128]{1,0:T(1,128)} %bitcast.4, s32[1,128]{1,0:T(1,128)} %bitcast.5, s32[2,128]{1,0:T(2,128)} %bitcast.3, bf16[4,1024]{1,0:T(4,128)(2,1)} %comps_hbm.1, bf16[4,64]{1,0:T(4,128)(2,1)} %gates_hbm.1, ...), custom_call_target="tpu_custom_call" | custom-call | tf_op jit(solution)/shard_map/pallas_call | solution.py:601
  74.4 0.6 copy.16
  75.0 0.8 %copy.17 = f32[128,1024]{1,0:T(8,128)} copy(f32[128,1024]{1,0:T(8,128)S(1)} %get-tuple-element.9) | data formatting | bytes 1048576
  75.8 0.6 copy.18
  76.4 0.6 copy.19

commit v4 on v3

--- a/solution.py
+++ b/solution.py
@@ -108,8 +108,24 @@
     for load in loads:
         load.start()
     barrier = pltpu.get_barrier_semaphore()
-    loop(1, shards, lambda k: pl.semaphore_signal(
-        barrier, inc=1, device_id=(g, lax.rem(s + k, shards)), device_id_type=MESH))
+    column = nx * CORES
+
+    def far_first(low, high, step):
+        def at_distance(turn):
+            away = (turn + 1) >> 1
+            z_to = lax.rem(z + nz // 2 + jnp.where((turn & 1) == 1, nz - away, away), nz)
+
+            def one(k):
+                p = z_to * column + k
+
+                @pl.when(p != s)
+                def _():
+                    step(p, z_to)
+            loop(0, column, one)
+        loop(low, high, at_distance)
+
+    far_first(0, nz, lambda p, z_to: pl.semaphore_signal(
+        barrier, inc=1, device_id=(g, p), device_id_type=MESH))
     loop(1, groups, lambda k: pl.semaphore_signal(
         barrier, inc=1, device_id=(lax.rem(g + k, groups), s), device_id_type=MESH))
 
@@ -149,8 +165,6 @@
 
     pl.semaphore_wait(barrier, shards - 1 + groups - 1)
 
-    column = nx * CORES
-
     def head(away, p):
         return pltpu.make_async_remote_copy(
             src_ref=head_send.at[p], dst_ref=head_recv.at[s],
@@ -158,15 +172,16 @@
             device_id=(g, p), device_id_type=MESH,
         )
 
-    def send_head(k):
-        p = lax.rem(s + k, shards)
-        head(lax.rem(z - lax.div(p, column) + nz, nz), p).start()
-    loop(1, shards, send_head)
+    far_first(0, nz, lambda p, z_to: head(lax.rem(z - z_to + nz, nz), p).start())
     head_recv[s] = head_send[s]
 
     def send_users(k):
         p = lax.rem(chip + k, chips)
-        copy(1, own_users, users_all.at[block(own, BLOCK)], (g, p * CORES + core)).start()
+        ahead = lax.rem(lax.div(p, nx) - z + nz, nz)
+
+        @pl.when((ahead <= 2) | (ahead >= nz - 2))
+        def _():
+            copy(1, own_users, users_all.at[block(own, BLOCK)], (g, p * CORES + core)).start()
         copy(17, own_gates, gates_all.at[pl.ds(own * gate_rows, gate_rows)], (g, p * CORES + core)).start()
     loop(1, chips, send_users)
     loads[5].wait()
@@ -192,6 +207,23 @@
         embedded[block(q, n), :] = (pre * share).astype(BF16)
         slope[:, columns] = share + pre * (0.3989422804014327 * jnp.exp(-0.5 * pre * pre))
     loop(0, QUARTERS, tower)
+
+    direct = min(5, nz) * nx - 1
+    wait_recv(1, users_all.at[pl.ds(0, direct * BLOCK)])
+
+    def relay(z_from, z_to, x_low, x_high):
+        def one(k):
+            here = block(core * chips + k * nz + z_from, BLOCK)
+            copy(19, users_all.at[here], users_all.at[here], at(z_to, x, core)).start()
+        loop(x_low, x_high, one)
+
+    relayed = (nz - min(5, nz)) * nx
+    if relayed:
+        up, down = lax.rem(z + 2, nz), lax.rem(z + nz - 2, nz)
+        relay(down, lax.rem(z + 1, nz), 0, nx)
+        relay(up, lax.rem(z + nz - 1, nz), 0, nx)
+        relay(down, up, 0, nx // 2)
+        relay(up, down, nx // 2, nx)
 
     tile_rows = min(256, rows)
     span = column * BLOCK
@@ -236,8 +268,8 @@
     loop(0, nz, answer)
     rows_recv[block(s, BLOCK), :] = rows_send[block(s, BLOCK), :]
 
-    others = pl.ds(0, half - BLOCK)
-    wait_recv(1, users_all.at[others])
+    if relayed:
+        wait_recv(19, users_all.at[pl.ds(0, relayed * BLOCK)])
     mine = pl.ds(pl.multiple_of(core * half, half), half)
     copy(4, users_all.at[mine], users_all.at[mine], partner).start()
     other_gates = pl.ds(0, (chips - 1) * gate_rows)
@@ -392,18 +424,9 @@
 
     far = max(1, 3 * nz // 8)
 
-    def send_back(step):
-        away = (step + 1) >> 1
-        z_to = lax.rem(z + nz // 2 + jnp.where((step & 1) == 1, nz - away, away), nz)
-
-        def send_one(k):
-            p = z_to * column + k
-
-            @pl.when(p != s)
-            def _():
-                copy(6, back_send.at[block(p, BLOCK)], back_recv.at[block(s, BLOCK)], (g, p)).start()
-        loop(0, column, send_one)
-    loop(0, far, send_back)
+    def send_back(p, z_to):
+        copy(6, back_send.at[block(p, BLOCK)], back_recv.at[block(s, BLOCK)], (g, p)).start()
+    far_first(0, far, send_back)
     back_recv[block(s, BLOCK), :] = back_send[block(s, BLOCK), :]
 
     def squeeze(i):
@@ -447,7 +470,7 @@
         to = lax.rem(z + k, nz)
         copy(10, tower_mid.at[block(to, depth)], tower_z.at[z], at(to, x, core)).start()
     loop(1, nz, send_z)
-    loop(far, nz, send_back)
+    far_first(far, nz, send_back)
 
     wait_recv(13, other_y.at[pl.ds(0, groups - 1)])
     total = other_part[block(g, deep), :].astype(F32)
@@ -544,7 +567,9 @@
     wait_send(14, other_x.at[pl.ds(0, nx - 1)])
 
     wait_send(0, head_send.at[pl.ds(0, shards - 1)])
-    wait_send(1, users_all.at[others])
+    wait_send(1, users_all.at[pl.ds(0, direct * BLOCK)])
+    if relayed:
+        wait_send(19, users_all.at[pl.ds(0, relayed * BLOCK)])
     wait_send(17, gates_all.at[other_gates])
     wait_send(18, gates_all.at[my_gates])
     wait_send(2, xt_recv)
@@ -609,7 +634,7 @@
         in_specs=[pl.BlockSpec(memory_space=pltpu.HBM)] * 8,
         out_specs=(whole,) * 4,
         scratch_shapes=[pltpu.VMEM(shape, kind) for shape, kind in scratch]
-        + [pltpu.SemaphoreType.DMA((19,)), pltpu.SemaphoreType.DMA((19,)), pltpu.SemaphoreType.DMA((nz,)),
+        + [pltpu.SemaphoreType.DMA((20,)), pltpu.SemaphoreType.DMA((20,)), pltpu.SemaphoreType.DMA((nz,)),
            pltpu.SemaphoreType.DMA((8,))],
         compiler_params=pltpu.CompilerParams(
             collective_id=0, has_side_effects=True, vmem_limit_bytes=32 * 1024 * 1024),

time: 77.1 us -> 79.8 us (1.035)
  Pallas kernels: 73.8 us -> 76.4 us
    pallas_call x1, Pallas kernels: 73.8 us -> 76.4 us  [local(): pl.pallas_call(functools.partial(kernel, groups, shards, nx), out_shape=(...]
where the time goes in v4:
time: 79.8 us; the launch traced here: 79.6 us
  Pallas kernels  76.4 us (96%)
  local copies, waits for them, and re-layouts  2.61 us (3%)
    pallas_call x1, Pallas kernels, local(): pl.pallas_call(functools.partial(kernel, groups, shards, nx), out_shape=(...  76.4 us
    unnamed x4, local copies, waits for them, and re-layouts  2.61 us

profile of v4, /device:TPU:32, one launch (start us, length us, event | category | flops | bytes accessed | tf_op | source)
XLA Modules:
  0.0 79.6 jit_solution(11491827036329346310)
XLA Ops:
  0.6 76.4 %shard_map.111 = (f32[16,1024]{1,0:T(8,128)S(1)}, f32[128,1024]{1,0:T(8,128)S(1)}, f32[4,1024]{1,0:T(4,128)S(1)}, f32[4,64]{1,0:T(4,128)S(1)}) custom-call(s32[1,128]{1,0:T(1,128)} %bitcast.4, s32[1,128]{1,0:T(1,128)} %bitcast.5, s32[2,128]{1,0:T(2,128)} %bitcast.3, bf16[4,1024]{1,0:T(4,128)(2,1)} %comps_hbm.1, bf16[4,64]{1,0:T(4,128)(2,1)} %gates_hbm.1, ...), custom_call_target="tpu_custom_call" | custom-call | tf_op jit(solution)/shard_map/pallas_call | solution.py:626
  77.0 0.6 copy.16
  77.7 0.8 copy.17
  78.5 0.6 copy.18
  79.1 0.6 copy.19

commit v5 on v3

--- a/solution.py
+++ b/solution.py
@@ -572,7 +572,7 @@
     half = rows // CORES
     depth = d // shards
     across = width + LANES
-    first = d * 5 // 8
+    first = d // 2
     other = d - first
     assert groups == nz
     scratch = [

time: 77.1 us -> 76.7 us (level)
  no operation moved by 1% of the time
where the time goes in v5:
time: 76.7 us; the launch traced here: 76.6 us
  Pallas kernels  73.4 us (96%)
  local copies, waits for them, and re-layouts  2.61 us (3%)
    pallas_call x1, Pallas kernels, local(): pl.pallas_call(functools.partial(kernel, groups, shards, nx), out_shape=(...  73.4 us
    unnamed x4, local copies, waits for them, and re-layouts  2.61 us

profile of v5, /device:TPU:32, one launch (start us, length us, event | category | flops | bytes accessed | tf_op | source)
XLA Modules:
  0.0 76.6 jit_solution(3384064369743153872)
XLA Ops:
  0.6 73.4 %shard_map.111 = (f32[16,1024]{1,0:T(8,128)S(1)}, f32[128,1024]{1,0:T(8,128)S(1)}, f32[4,1024]{1,0:T(4,128)S(1)}, f32[4,64]{1,0:T(4,128)S(1)}) custom-call(s32[1,128]{1,0:T(1,128)} %bitcast.4, s32[1,128]{1,0:T(1,128)} %bitcast.5, s32[2,128]{1,0:T(2,128)} %bitcast.3, bf16[4,1024]{1,0:T(4,128)(2,1)} %comps_hbm.1, bf16[4,64]{1,0:T(4,128)(2,1)} %gates_hbm.1, ...), custom_call_target="tpu_custom_call" | custom-call | tf_op jit(solution)/shard_map/pallas_call | solution.py:601
  74.0 0.6 copy.16
  74.6 0.8 %copy.17 = f32[128,1024]{1,0:T(8,128)} copy(f32[128,1024]{1,0:T(8,128)S(1)} %get-tuple-element.9) | data formatting | bytes 1048576
  75.4 0.6 copy.18
  76.0 0.6 copy.19
